TPU v7x, 256 devices: a whole 4x4x8 slice. The times are simulated.
256 devices in a mesh: grp: 2 (over core), tile: 128 (over z, y, x).
Axes of the slice: x: 4, y: 4, z: 8, core: 2. Of those that a mesh axis runs over, the one named last changes fastest.
Arguments:
- source_points: float32 [2, 3, 4194304], P('grp', None, 'tile'), may hold values from -6 to 6
- intersection: int32 [2, 16384, 1], P('grp', 'tile'), may hold values from 0 to 127; in each aligned block of 128 rows (0 to 127, 128 to 255, ..., all dimensions but the last counted through in order) at most 2 rows name the same one
- target_scan: int32 [2, 16384], P('grp', 'tile'), may hold values from 0 to 63
- matches: int32 [2, 4194304], P('grp', 'tile'), may hold values from 0 to 511
- target_points: float32 [3, 4194304], P(None, 'tile'), may hold values from -6 to 6
- target_normals: float32 [3, 4194304], P(None, 'tile'), may hold values from -4 to 4
Outputs:
- pose_step: float32 [6, 8192], P(None, 'tile')
Inputs may be any that keep to these rules, and one draw needn't show every extreme that they name: `intersection`: within the blocks of one device (each aligned run of 128 rows), no index is named more than 2 times, a bound that some block reaches.
All inputs are finite; a program needn't handle non-finite values.
Results may differ from a plain program's by a relative error of at most 0.0003.
Values sent between devices are 32-bit elements; how exact they have to be, the bound alone decides.
A program may use at most 64 MiB of HBM per device.

v0:
```python
import math

import jax
import jax.numpy as jnp
from jax import lax
from jax.sharding import PartitionSpec as P

SCANS_DEV = 64
TARGET_PTS = 512


DAMPING = 0.1
PRECISE = lax.Precision.HIGHEST


def over_pieces(shard, axis):
    return lax.all_gather(shard, axis).sum(0)


def cross_rows(first_vec, second_vec):
    return jnp.stack(
        [
            first_vec[1] * second_vec[2] - first_vec[2] * second_vec[1],
            first_vec[2] * second_vec[0] - first_vec[0] * second_vec[2],
            first_vec[0] * second_vec[1] - first_vec[1] * second_vec[0],
        ]
    )


def pair_terms(source, target, normal, usable):
    jacobian = (
        jnp.concatenate(
            [cross_rows(source, normal), normal, -cross_rows(target, normal), -normal], axis=0
        )
        * usable[None]
    )
    misfit = jnp.sum(normal * (source - target), axis=0) * usable
    normal_blocks = jnp.einsum("anks,bnks->abnk", jacobian, jacobian, precision=PRECISE)
    gradient = jnp.einsum("anks,nks->ank", jacobian, misfit, precision=PRECISE)
    layout = jacobian.shape[1:3]
    own_terms = jnp.concatenate(
        [normal_blocks[:6, :6].reshape((36,) + layout), gradient[:6]], axis=0
    )
    theirs = jnp.concatenate([normal_blocks[6:, 6:].reshape((36,) + layout), gradient[6:]], axis=0)
    return (own_terms, theirs)


def solve_poses(scan_totals):
    entries = [[scan_totals[6 * row_at + col_at] for col_at in range(6)] for row_at in range(6)]
    traced = entries[0][0]
    for step_at in range(1, 6):
        traced = traced + entries[step_at][step_at]
    shift_by = DAMPING * traced / 6.0
    for step_at in range(6):
        entries[step_at][step_at] = entries[step_at][step_at] + shift_by
    values = [-scan_totals[36 + row_at] for row_at in range(6)]
    for pivot_at in range(6):
        for row_at in range(pivot_at + 1, 6):
            factor = entries[row_at][pivot_at] / entries[pivot_at][pivot_at]
            for col_at in range(pivot_at, 6):
                entries[row_at][col_at] = (
                    entries[row_at][col_at] - factor * entries[pivot_at][col_at]
                )
            values[row_at] = values[row_at] - factor * values[pivot_at]
    result = [None] * 6
    for row_at in range(5, -1, -1):
        running = values[row_at]
        for col_at in range(row_at + 1, 6):
            running = running - entries[row_at][col_at] * result[col_at]
        result[row_at] = running / entries[row_at][row_at]
    return jnp.stack(result)


def body(source_points, intersection, target_scan, matches, target_points, target_normals):
    tile_count = lax.axis_size("tile")
    blocks = intersection.shape[1]
    capacity = 2 * blocks // tile_count
    slot_count = tile_count * capacity
    points = source_points.shape[2] // blocks
    per_scan = blocks // SCANS_DEV
    destin = intersection[0, :, 0]
    block_range = jnp.arange(blocks, dtype=jnp.int32)
    onehot_dest = (destin[:, None] == jnp.arange(tile_count, dtype=jnp.int32)[None, :]).astype(
        jnp.float32
    )
    lower = (block_range[:, None] >= block_range[None, :]).astype(jnp.float32)
    running = jnp.dot(lower, onehot_dest, precision=PRECISE)
    ranked = jnp.sum(running * onehot_dest, axis=1).astype(jnp.int32) - 1
    slot_of = destin * capacity + ranked
    placing = (slot_of[None, :] == jnp.arange(slot_count, dtype=jnp.int32)[:, None]).astype(
        jnp.float32
    )
    filled = jnp.sum(placing, axis=1) > 0.5
    safe_block = jnp.dot(placing, block_range.astype(jnp.float32), precision=PRECISE).astype(
        jnp.int32
    )
    shaped = (tile_count, capacity, points)
    coords = source_points[0].reshape(3, blocks, points)
    packed = jnp.einsum("sb,cbk->csk", placing, coords, precision=PRECISE).reshape((3,) + shaped)
    wanted = (target_scan[0][:, None] * TARGET_PTS + matches[0].reshape(blocks, points)).astype(
        jnp.float32
    )
    placed = jnp.dot(placing, wanted, precision=PRECISE).astype(jnp.int32)
    request = jnp.where(filled[:, None], placed, -1).reshape((1,) + shaped)
    tables = jnp.concatenate([target_points, target_normals], axis=0).reshape(
        6, SCANS_DEV, TARGET_PTS
    )
    tables = jnp.transpose(tables, (1, 0, 2)).reshape(SCANS_DEV, 6 * TARGET_PTS)
    scan_range = jnp.arange(SCANS_DEV, dtype=jnp.int32)
    column_range = jnp.arange(TARGET_PTS, dtype=jnp.int32)
    outgoing = jnp.concatenate([packed, request.astype(jnp.float32)], axis=0)
    incoming = lax.all_to_all(outgoing, "tile", split_axis=1, concat_axis=1, tiled=True)
    target_index = incoming[3:].astype(jnp.int32)
    lookup_target_index = target_index[0]
    outer = lookup_target_index.shape[:-1]
    width = lookup_target_index.shape[-1]
    items = math.prod(outer)
    flat = jnp.maximum(lookup_target_index, 0).reshape(items, width)
    item_scan = flat[:, 0] // TARGET_PTS
    within = flat % TARGET_PTS
    scan_pick = (item_scan[:, None] == scan_range[None, :]).astype(jnp.float32)
    block_tables = jnp.dot(scan_pick, tables, precision=PRECISE).reshape(items, 6, TARGET_PTS)
    group = math.gcd(items, 16)

    def select(pair):
        table_part, column_part = pair
        chooser = (column_part[:, None, :] == column_range[None, :, None]).astype(jnp.float32)
        return jnp.einsum("icj,ijk->ick", table_part, chooser, precision=PRECISE)

    picked = lax.map(
        select,
        (
            block_tables.reshape(items // group, group, 6, TARGET_PTS),
            within.reshape(items // group, group, width),
        ),
    )
    picked = jnp.transpose(picked.reshape(items, 6, width), (1, 0, 2)).reshape(
        (6,) + outer + (width,)
    )
    nearest = picked[:3]
    facing = picked[3:]
    usable = (target_index[0] >= 0).astype(jnp.float32)
    mine, far_terms = pair_terms(incoming[:3], nearest, facing, usable)
    returned = lax.all_to_all(mine, "tile", split_axis=1, concat_axis=1, tiled=True)
    leading = target_index[:, :, :, 0]
    owner_scan = jnp.where(leading >= 0, leading // TARGET_PTS, -1)
    source_scan = jnp.where(filled, safe_block // per_scan, -1)
    src_onehot = (source_scan[None, :] == scan_range[:, None]).astype(jnp.float32)
    tgt_onehot = (owner_scan.reshape(slot_count)[None, :] == scan_range[:, None]).astype(
        jnp.float32
    )
    local_sums = jnp.dot(returned.reshape(42, slot_count), src_onehot.T, precision=PRECISE)
    local_sums = local_sums + jnp.dot(
        far_terms.reshape(42, slot_count), tgt_onehot.T, precision=PRECISE
    )
    totals = over_pieces(local_sums, "grp")
    return solve_poses(totals)


def solution(mesh):
    in_specs = (
        P("grp", None, "tile"),
        P("grp", "tile", None),
        P("grp", "tile"),
        P("grp", "tile"),
        P(None, "tile"),
        P(None, "tile"),
    )
    out_specs = P(None, "tile")
    return jax.shard_map(body, mesh=mesh, in_specs=in_specs, out_specs=out_specs, check_vma=False)
```

profile of v0, /device:TPU:1, one launch (start us, length us, event | category | flops | bytes accessed | tf_op | source)
XLA Modules:
  0.0 199.2 jit_solution(6584830246654573177)
XLA Ops:
  3.1 1.8 reduce.7
  5.5 2.1 %reduce.1 = f32[3,32768]{1,0:T(4,128)S(1)} reduce(f32[1,3,32768]{2,0,1:T(1,128)} %param.8, f32[]{:T(128)} %constant.83), dimensions={0}, to_apply=%param.8.reduce_sub_computation | reduce | bytes 786436 | tf_op args[0]
  9.1 1.3 copy.157
  10.4 16.3 %all-to-all-start = ((f32[4,128,2,256]{3,2,0,1:T(2,128)}), f32[4,128,2,256]{3,2,0,1:T(2,128)S(1)}, u32[]{:S(2)}, u32[]{:S(2)}) async-start(f32[4,128,2,256]{3,2,0,1:T(2,128)} %copy.157), calls=%async_computation | async-start | bytes 2097152 | tf_op jit(solution)/shard_map/all_to_all | solution.py:112
  27.0 28.5 %all-to-all-done = f32[4,128,2,256]{3,2,0,1:T(2,128)S(1)} async-done(((f32[4,128,2,256]{3,2,0,1:T(2,128)}), f32[4,128,2,256]{3,2,0,1:T(2,128)S(1)}, u32[]{:S(2)}, u32[]{:S(2)}) %all-to-all-start) | async-done | bytes 1048608 | tf_op jit(solution)/shard_map/all_to_all | solution.py:112
  55.5 1.1 fusion.105
  58.6 3.4 %fusion.17 = f32[16,16,6,512]{3,1,2,0:T(8,128)} fusion(s32[16,16]{1,0:T(8,128)S(1)} %eq.103, f32[8,8,6,512]{3,2,1,0:T(8,128)S(1)} %bitcast.83), kind=kOutput, calls=%fused_computation.27 | convolution fusion | flops 603996160 | bytes 3933184 | tf_op jit(solution)/shard_map/dot_general | solution.py:122
  62.0 69.7 %while.11 = (s32[]{:T(128)}, f32[16,16,6,256]{3,2,1,0:T(8,128)}, f32[16,16,6,512]{3,1,2,0:T(8,128)}, s32[16,16,256]{2,1,0:T(8,128)S(1)}, s32[]{:T(128)}) while((s32[]{:T(128)}, f32[16,16,6,256]{3,2,1,0:T(8,128)}, f32[16,16,6,512]{3,1,2,0:T(8,128)}, s32[16,16,256]{2,1,0:T(8,128)S(1)}, s32[]{:T(128)}) %tuple.80), condition=%wide.region_3.4_spmd.clone, body=%wide.region_2.3_spmd.clone.sunk | while | flops 153092096 | bytes 770129 | solution.py:130
  62.9 3.4 %fusion.109 = f32[16,16,6,256]{3,2,1,0:T(8,128)} fusion(f32[16,16,6,256]{3,2,1,0:T(8,128)} %get-tuple-element.179, s32[]{:T(128)S(6)} %copy.288, s32[16,256]{1,0:T(8,128)S(1)} %dynamic-slice_bitcast_fusion.2, f32[1,16,6,512]{3,1,2,0:T(8,128)S(1)} %constant_dynamic-slice_fusion.2), kind=kOutput, calls=%fused_computation.5.clone.1 | convolution fusion | flops 153092096 | bytes 344068 | tf_op jit(solution)/shard_map/while/body/eval_jaxpr/icj,ijk->ick/dot_general | solution.py:128
  67.3 3.4 %fusion.109 = f32[16,16,6,256]{3,2,1,0:T(8,128)} fusion(f32[16,16,6,256]{3,2,1,0:T(8,128)} %get-tuple-element.179, s32[]{:T(128)S(6)} %copy.288, s32[16,256]{1,0:T(8,128)S(1)} %dynamic-slice_bitcast_fusion.2, f32[1,16,6,512]{3,1,2,0:T(8,128)S(1)} %constant_dynamic-slice_fusion.2), kind=kOutput, calls=%fused_computation.5.clone.1 | convolution fusion | flops 153092096 | bytes 344068 | tf_op jit(solution)/shard_map/while/body/eval_jaxpr/icj,ijk->ick/dot_general | solution.py:128
  71.6 3.4 %fusion.109 = f32[16,16,6,256]{3,2,1,0:T(8,128)} fusion(f32[16,16,6,256]{3,2,1,0:T(8,128)} %get-tuple-element.179, s32[]{:T(128)S(6)} %copy.288, s32[16,256]{1,0:T(8,128)S(1)} %dynamic-slice_bitcast_fusion.2, f32[1,16,6,512]{3,1,2,0:T(8,128)S(1)} %constant_dynamic-slice_fusion.2), kind=kOutput, calls=%fused_computation.5.clone.1 | convolution fusion | flops 153092096 | bytes 344068 | tf_op jit(solution)/shard_map/while/body/eval_jaxpr/icj,ijk->ick/dot_general | solution.py:128
  76.0 3.4 %fusion.109 = f32[16,16,6,256]{3,2,1,0:T(8,128)} fusion(f32[16,16,6,256]{3,2,1,0:T(8,128)} %get-tuple-element.179, s32[]{:T(128)S(6)} %copy.288, s32[16,256]{1,0:T(8,128)S(1)} %dynamic-slice_bitcast_fusion.2, f32[1,16,6,512]{3,1,2,0:T(8,128)S(1)} %constant_dynamic-slice_fusion.2), kind=kOutput, calls=%fused_computation.5.clone.1 | convolution fusion | flops 153092096 | bytes 344068 | tf_op jit(solution)/shard_map/while/body/eval_jaxpr/icj,ijk->ick/dot_general | solution.py:128
  80.3 3.4 %fusion.109 = f32[16,16,6,256]{3,2,1,0:T(8,128)} fusion(f32[16,16,6,256]{3,2,1,0:T(8,128)} %get-tuple-element.179, s32[]{:T(128)S(6)} %copy.288, s32[16,256]{1,0:T(8,128)S(1)} %dynamic-slice_bitcast_fusion.2, f32[1,16,6,512]{3,1,2,0:T(8,128)S(1)} %constant_dynamic-slice_fusion.2), kind=kOutput, calls=%fused_computation.5.clone.1 | convolution fusion | flops 153092096 | bytes 344068 | tf_op jit(solution)/shard_map/while/body/eval_jaxpr/icj,ijk->ick/dot_general | solution.py:128
  84.7 3.4 %fusion.109 = f32[16,16,6,256]{3,2,1,0:T(8,128)} fusion(f32[16,16,6,256]{3,2,1,0:T(8,128)} %get-tuple-element.179, s32[]{:T(128)S(6)} %copy.288, s32[16,256]{1,0:T(8,128)S(1)} %dynamic-slice_bitcast_fusion.2, f32[1,16,6,512]{3,1,2,0:T(8,128)S(1)} %constant_dynamic-slice_fusion.2), kind=kOutput, calls=%fused_computation.5.clone.1 | convolution fusion | flops 153092096 | bytes 344068 | tf_op jit(solution)/shard_map/while/body/eval_jaxpr/icj,ijk->ick/dot_general | solution.py:128
  89.0 3.4 %fusion.109 = f32[16,16,6,256]{3,2,1,0:T(8,128)} fusion(f32[16,16,6,256]{3,2,1,0:T(8,128)} %get-tuple-element.179, s32[]{:T(128)S(6)} %copy.288, s32[16,256]{1,0:T(8,128)S(1)} %dynamic-slice_bitcast_fusion.2, f32[1,16,6,512]{3,1,2,0:T(8,128)S(1)} %constant_dynamic-slice_fusion.2), kind=kOutput, calls=%fused_computation.5.clone.1 | convolution fusion | flops 153092096 | bytes 344068 | tf_op jit(solution)/shard_map/while/body/eval_jaxpr/icj,ijk->ick/dot_general | solution.py:128
  93.4 3.4 %fusion.109 = f32[16,16,6,256]{3,2,1,0:T(8,128)} fusion(f32[16,16,6,256]{3,2,1,0:T(8,128)} %get-tuple-element.179, s32[]{:T(128)S(6)} %copy.288, s32[16,256]{1,0:T(8,128)S(1)} %dynamic-slice_bitcast_fusion.2, f32[1,16,6,512]{3,1,2,0:T(8,128)S(1)} %constant_dynamic-slice_fusion.2), kind=kOutput, calls=%fused_computation.5.clone.1 | convolution fusion | flops 153092096 | bytes 344068 | tf_op jit(solution)/shard_map/while/body/eval_jaxpr/icj,ijk->ick/dot_general | solution.py:128
  97.7 3.4 %fusion.109 = f32[16,16,6,256]{3,2,1,0:T(8,128)} fusion(f32[16,16,6,256]{3,2,1,0:T(8,128)} %get-tuple-element.179, s32[]{:T(128)S(6)} %copy.288, s32[16,256]{1,0:T(8,128)S(1)} %dynamic-slice_bitcast_fusion.2, f32[1,16,6,512]{3,1,2,0:T(8,128)S(1)} %constant_dynamic-slice_fusion.2), kind=kOutput, calls=%fused_computation.5.clone.1 | convolution fusion | flops 153092096 | bytes 344068 | tf_op jit(solution)/shard_map/while/body/eval_jaxpr/icj,ijk->ick/dot_general | solution.py:128
  102.1 3.4 %fusion.109 = f32[16,16,6,256]{3,2,1,0:T(8,128)} fusion(f32[16,16,6,256]{3,2,1,0:T(8,128)} %get-tuple-element.179, s32[]{:T(128)S(6)} %copy.288, s32[16,256]{1,0:T(8,128)S(1)} %dynamic-slice_bitcast_fusion.2, f32[1,16,6,512]{3,1,2,0:T(8,128)S(1)} %constant_dynamic-slice_fusion.2), kind=kOutput, calls=%fused_computation.5.clone.1 | convolution fusion | flops 153092096 | bytes 344068 | tf_op jit(solution)/shard_map/while/body/eval_jaxpr/icj,ijk->ick/dot_general | solution.py:128
  106.4 3.4 %fusion.109 = f32[16,16,6,256]{3,2,1,0:T(8,128)} fusion(f32[16,16,6,256]{3,2,1,0:T(8,128)} %get-tuple-element.179, s32[]{:T(128)S(6)} %copy.288, s32[16,256]{1,0:T(8,128)S(1)} %dynamic-slice_bitcast_fusion.2, f32[1,16,6,512]{3,1,2,0:T(8,128)S(1)} %constant_dynamic-slice_fusion.2), kind=kOutput, calls=%fused_computation.5.clone.1 | convolution fusion | flops 153092096 | bytes 344068 | tf_op jit(solution)/shard_map/while/body/eval_jaxpr/icj,ijk->ick/dot_general | solution.py:128
  110.8 3.4 %fusion.109 = f32[16,16,6,256]{3,2,1,0:T(8,128)} fusion(f32[16,16,6,256]{3,2,1,0:T(8,128)} %get-tuple-element.179, s32[]{:T(128)S(6)} %copy.288, s32[16,256]{1,0:T(8,128)S(1)} %dynamic-slice_bitcast_fusion.2, f32[1,16,6,512]{3,1,2,0:T(8,128)S(1)} %constant_dynamic-slice_fusion.2), kind=kOutput, calls=%fused_computation.5.clone.1 | convolution fusion | flops 153092096 | bytes 344068 | tf_op jit(solution)/shard_map/while/body/eval_jaxpr/icj,ijk->ick/dot_general | solution.py:128
  115.2 3.4 %fusion.109 = f32[16,16,6,256]{3,2,1,0:T(8,128)} fusion(f32[16,16,6,256]{3,2,1,0:T(8,128)} %get-tuple-element.179, s32[]{:T(128)S(6)} %copy.288, s32[16,256]{1,0:T(8,128)S(1)} %dynamic-slice_bitcast_fusion.2, f32[1,16,6,512]{3,1,2,0:T(8,128)S(1)} %constant_dynamic-slice_fusion.2), kind=kOutput, calls=%fused_computation.5.clone.1 | convolution fusion | flops 153092096 | bytes 344068 | tf_op jit(solution)/shard_map/while/body/eval_jaxpr/icj,ijk->ick/dot_general | solution.py:128
  119.5 3.4 %fusion.109 = f32[16,16,6,256]{3,2,1,0:T(8,128)} fusion(f32[16,16,6,256]{3,2,1,0:T(8,128)} %get-tuple-element.179, s32[]{:T(128)S(6)} %copy.288, s32[16,256]{1,0:T(8,128)S(1)} %dynamic-slice_bitcast_fusion.2, f32[1,16,6,512]{3,1,2,0:T(8,128)S(1)} %constant_dynamic-slice_fusion.2), kind=kOutput, calls=%fused_computation.5.clone.1 | convolution fusion | flops 153092096 | bytes 344068 | tf_op jit(solution)/shard_map/while/body/eval_jaxpr/icj,ijk->ick/dot_general | solution.py:128
  123.9 3.4 %fusion.109 = f32[16,16,6,256]{3,2,1,0:T(8,128)} fusion(f32[16,16,6,256]{3,2,1,0:T(8,128)} %get-tuple-element.179, s32[]{:T(128)S(6)} %copy.288, s32[16,256]{1,0:T(8,128)S(1)} %dynamic-slice_bitcast_fusion.2, f32[1,16,6,512]{3,1,2,0:T(8,128)S(1)} %constant_dynamic-slice_fusion.2), kind=kOutput, calls=%fused_computation.5.clone.1 | convolution fusion | flops 153092096 | bytes 344068 | tf_op jit(solution)/shard_map/while/body/eval_jaxpr/icj,ijk->ick/dot_general | solution.py:128
  128.2 3.4 %fusion.109 = f32[16,16,6,256]{3,2,1,0:T(8,128)} fusion(f32[16,16,6,256]{3,2,1,0:T(8,128)} %get-tuple-element.179, s32[]{:T(128)S(6)} %copy.288, s32[16,256]{1,0:T(8,128)S(1)} %dynamic-slice_bitcast_fusion.2, f32[1,16,6,512]{3,1,2,0:T(8,128)S(1)} %constant_dynamic-slice_fusion.2), kind=kOutput, calls=%fused_computation.5.clone.1 | convolution fusion | flops 153092096 | bytes 344068 | tf_op jit(solution)/shard_map/while/body/eval_jaxpr/icj,ijk->ick/dot_general | solution.py:128
  131.6 2.1 %copy.282 = f32[256,6,256]{2,0,1:T(8,128)S(1)} copy(f32[256,6,256]{2,1,0:T(8,128)} %bitcast.84) | data formatting | bytes 3145728 | tf_op jit(solution)/shard_map/reshape | solution.py:137
  133.7 1.0 fusion.104
  134.8 1.9 squeeze.27
  136.8 1.3 slice.235
  138.1 1.2 squeeze.25
  139.3 1.2 squeeze.24
  140.5 1.9 squeeze.23
  142.4 1.0 squeeze.28
  144.9 2.5 %multiply_subtract_fusion.2 = (f32[1,128,2,256]{3,1,2,0:T(8,128)}, f32[12,128,2,256]{3,1,2,0:T(8,128)}, f32[1,128,2,256]{3,1,2,0:T(8,128)}, f32[1,128,2,256]{3,1,2,0:T(8,128)}, s32[1,128,2,256]{3,1,2,0:T(8,128)S(1)}) fusion(f32[1,128,2,256]{3,0,2,1:T(1,128)} %squeeze.27, f32[1,128,2,256]{3,0,2,1:T(1,128)} %squeeze.26, f32[1,128,2,256]{3,0,2,1:T(1,128)S(1)} %squeeze.24, ...), kind=kLoop, calls=%fused_computation.45 | loop fusion | flops 851967 | bytes 3670016 | tf_op jit(solution)/shard_map/sub | solution.py:23
  147.4 1.5 copy.201
  148.9 1.0 squeeze.29
  149.9 1.8 subtract_dynamic-update-slice_fusion.1
  151.6 1.8 subtract_dynamic-update-slice_fusion
  153.4 1.0 copy_dynamic-update-slice_fusion
  155.7 1.1 fusion.21
  156.7 2.1 %broadcast_multiply_fusion = f32[12,128,2,256]{3,1,2,0:T(8,128)S(1)} fusion(f32[12,128,2,256]{3,1,2,0:T(8,128)} %get-tuple-element.138, f32[128,2,256]{2,0,1:T(8,128)S(1)} %copy-done.7), kind=kLoop, calls=%fused_computation.15 | loop fusion | flops 786432 | bytes 6553600 | tf_op jit(solution)/shard_map/mul | solution.py:32
  158.9 5.6 %fusion.10 = f32[12,12,128,2]{0,1,3,2:T(8,128)S(1)} fusion(f32[12,128,2,256]{3,1,2,0:T(8,128)S(1)} %broadcast_multiply_fusion), kind=kOutput, calls=%fused_computation.13 | convolution fusion | flops 113246208 | bytes 3293184 | tf_op jit(solution)/shard_map/anks,bnks->abnk/dot_general | solution.py:38
  164.8 6.0 %fusion.6 = f32[128,2,1,12]{3,2,1,0:T(1,128)S(1)} fusion(f32[12,128,2,256]{3,1,2,0:T(8,128)S(1)} %broadcast_multiply_fusion, f32[128,2,256,1]{2,1,0,3:T(2,128)S(1)} %fusion.24), kind=kOutput, calls=%fused_computation.9 | convolution fusion | flops 9437184 | bytes 3420160 | tf_op jit(solution)/shard_map/anks,nks->ank/dot_general | solution.py:39
  170.9 1.3 fusion.102
  172.2 1.5 copy.190
  174.5 8.0 %all-to-all-start.1 = ((f32[42,128,2]{0,2,1:T(2,128)}), f32[42,128,2]{0,2,1:T(2,128)S(1)}, u32[]{:S(2)}, u32[]{:S(2)}) async-start(f32[42,128,2]{0,2,1:T(2,128)} %copy.196), calls=%async_computation.1 | async-start | bytes 262144 | tf_op jit(solution)/shard_map/all_to_all | solution.py:144
  182.5 1.7 copy.197
  184.8 9.0 %all-to-all-done.1 = f32[42,128,2]{0,2,1:T(2,128)S(1)} async-done(((f32[42,128,2]{0,2,1:T(2,128)}), f32[42,128,2]{0,2,1:T(2,128)S(1)}, u32[]{:S(2)}, u32[]{:S(2)}) %all-to-all-start.1) | async-done | bytes 43040 | tf_op jit(solution)/shard_map/all_to_all | solution.py:144
  194.2 4.3 %all-gather.1 = f32[2,42,64]{2,1,0:T(8,128)S(1)} all-gather(f32[1,42,64]{2,1,0:T(8,128)S(1)} %fusion.16), channel_id=2, replica_groups=mesh['grp'=2,'tile'=128] {'grp'}, dimensions={0}, use_global_device_ids=true | all-gather | bytes 32256 | tf_op jit(solution)/shard_map/all_gather | solution.py:17
  (102 shorter events, 28.0 us)
Async XLA Ops:
  8.6 18.2 %copy-start.8 = (f32[3,32768]{1,0:T(4,128)S(1)}, f32[3,32768]{1,0:T(4,128)}, u32[]{:S(2)}) copy-start(f32[3,32768]{1,0:T(4,128)} %param.13) | copy-start | bytes 1179652
  8.6 18.2 %copy-start.9 = (f32[3,32768]{1,0:T(4,128)S(1)}, f32[3,32768]{1,0:T(4,128)}, u32[]{:S(2)}) copy-start(f32[3,32768]{1,0:T(4,128)} %param.12) | copy-start | bytes 1179652
  10.4 45.1 %all-to-all-start = ((f32[4,128,2,256]{3,2,0,1:T(2,128)}), f32[4,128,2,256]{3,2,0,1:T(2,128)S(1)}, u32[]{:S(2)}, u32[]{:S(2)}) async-start(f32[4,128,2,256]{3,2,0,1:T(2,128)} %copy.157), calls=%async_computation | async-start | bytes 2097152 | tf_op jit(solution)/shard_map/all_to_all | solution.py:112
  144.9 5.0 %copy-start.1 = (f32[1,128,2,256]{3,0,2,1:T(1,128)S(1)}, f32[1,128,2,256]{3,0,2,1:T(1,128)}, u32[]{:S(2)}) copy-start(f32[1,128,2,256]{3,0,2,1:T(1,128)} %squeeze.23) | copy-start | bytes 786436
  144.9 5.0 %copy-start.3 = (f32[1,128,2,256]{3,2,0,1:T(2,128)S(1)}, f32[1,128,2,256]{3,2,0,1:T(2,128)}, u32[]{:S(2)}) copy-start(f32[1,128,2,256]{3,2,0,1:T(2,128)} %get-tuple-element.134) | copy-start | bytes 786436
  144.9 6.8 %copy-start.2 = (f32[1,128,2,256]{3,2,0,1:T(2,128)S(1)}, f32[1,128,2,256]{3,2,0,1:T(2,128)}, u32[]{:S(2)}) copy-start(f32[1,128,2,256]{3,2,0,1:T(2,128)} %get-tuple-element.136) | copy-start | bytes 786436
  147.4 7.0 %copy-start.4 = (f32[1,128,2,256]{3,1,2,0:T(8,128)S(1)}, f32[1,128,2,256]{3,1,2,0:T(8,128)}, u32[]{:S(2)}) copy-start(f32[1,128,2,256]{3,1,2,0:T(8,128)} %get-tuple-element.139) | copy-start | bytes 786436
  149.8 4.6 %copy-start.5 = (f32[1,128,2,256]{3,1,2,0:T(8,128)S(1)}, f32[1,128,2,256]{3,1,2,0:T(8,128)}, u32[]{:S(2)}) copy-start(f32[1,128,2,256]{3,1,2,0:T(8,128)} %get-tuple-element.141) | copy-start | bytes 786436
  149.8 4.6 %copy-start.6 = (f32[1,128,2,256]{3,1,2,0:T(8,128)S(1)}, f32[1,128,2,256]{3,1,2,0:T(8,128)}, u32[]{:S(2)}) copy-start(f32[1,128,2,256]{3,1,2,0:T(8,128)} %get-tuple-element.142) | copy-start | bytes 786436
  151.6 4.0 %copy-start = (f32[3,128,2,256]{3,2,1,0:T(2,128)S(1)}, f32[3,128,2,256]{3,2,1,0:T(2,128)}, u32[]{:S(2)}) copy-start(f32[3,128,2,256]{3,2,1,0:T(2,128)} %slice.235) | copy-start | bytes 2359300
  154.4 2.3 %copy-start.7 = (f32[128,2,256]{2,0,1:T(8,128)S(1)}, f32[128,2,256]{2,0,1:T(8,128)}, u32[]{:S(2)}) copy-start(f32[128,2,256]{2,0,1:T(8,128)} %get-tuple-element.121) | copy-start | bytes 786436
  158.9 5.7 %copy-start.10 = (pred[128,2,256]{2,0,1:T(8,128)(4,1)S(1)}, pred[128,2,256]{2,0,1:T(8,128)(4,1)}, u32[]{:S(2)}) copy-start(pred[128,2,256]{2,0,1:T(8,128)(4,1)} %get-tuple-element.122) | copy-start | bytes 196612
  174.5 19.2 %all-to-all-start.1 = ((f32[42,128,2]{0,2,1:T(2,128)}), f32[42,128,2]{0,2,1:T(2,128)S(1)}, u32[]{:S(2)}, u32[]{:S(2)}) async-start(f32[42,128,2]{0,2,1:T(2,128)} %copy.196), calls=%async_computation.1 | async-start | bytes 262144 | tf_op jit(solution)/shard_map/all_to_all | solution.py:144
where the time goes:
time: 200 us; the launch traced here: 199 us
  matrix products  71.8 us (36%)
  local copies, waits for them, and re-layouts  43.1 us (22%)
  waiting for transfers between devices  37.4 us (19%)
  starting transfers between devices  24.3 us (12%)
  other arithmetic  17.8 us (9%)
  blocking collectives  4.25 us (2%)
    dot_general x16, matrix products, select(): return jnp.einsum('icj,ijk->ick', table_part, chooser, precision=PRECISE)  54.5 us
    all_to_all x1, waiting for transfers between devices, body(): lax.all_to_all(outgoing, 'tile', split_axis=1, concat_axis=1, tiled=True)  28.5 us
    all_to_all x1, starting transfers between devices, body(): lax.all_to_all(outgoing, 'tile', split_axis=1, concat_axis=1, tiled=True)  16.3 us
    dynamic_slice x16, local copies, waits for them, and re-layouts, body(): lax.map(select, (block_tables.reshape(items // group, group, 6, TARGET_PT...  15 us
    all_to_all x1, waiting for transfers between devices, body(): lax.all_to_all(mine, 'tile', split_axis=1, concat_axis=1, tiled=True)  8.95 us
    unnamed x5, other arithmetic  8.4 us
    all_to_all x1, starting transfers between devices, body(): lax.all_to_all(mine, 'tile', split_axis=1, concat_axis=1, tiled=True)  7.97 us
    dot_general x1, matrix products, pair_terms(): gradient = jnp.einsum('anks,nks->ank', jacobian, misfit, precision=PRECISE)  5.96 us
  transfers between devices with their start and end apart: 2, of which 2 were waited for; matrix products, arithmetic and copies ran while one was open for 1% of the time, Pallas kernels for 0%

commit v1 on v0

v1 whole, which is shorter than its diff:
```python
import jax
import jax.numpy as jnp
from jax import lax
from jax.experimental import pallas as pl
from jax.experimental.pallas import tpu as pltpu
from jax.sharding import PartitionSpec as P

TILES = 128
SCANS_DEV = 64
TARGET_PTS = 512
LANES = 128
DAMPING = 0.1
PRECISE = lax.Precision.HIGHEST
F32 = jnp.float32
I32 = jnp.int32
DZ_ORDER = (4, 3, 5, 2, 6, 1, 7, 0)

PAIRS = [(i, j) for i in range(3) for j in range(i, 3)]
AT_AN, AT_AM, AT_NN, AT_NM, AT_B = 6, 15, 18, 24, 32


def parts_of(value):
    high = value.astype(jnp.bfloat16)
    rest = value - high.astype(F32)
    middle = rest.astype(jnp.bfloat16)
    low = (rest - middle.astype(F32)).astype(jnp.bfloat16)
    return high, middle, low


def solve_rows(rows):
    entries = [[None] * 6 for _ in range(6)]
    for at, (i, j) in enumerate(PAIRS):
        entries[i][j] = entries[j][i] = rows[at]
        entries[3 + i][3 + j] = entries[3 + j][3 + i] = rows[AT_NN + at]
    for i in range(3):
        for j in range(3):
            entries[i][3 + j] = entries[3 + j][i] = rows[AT_AN + 3 * i + j]
    traced = entries[0][0]
    for at in range(1, 6):
        traced = traced + entries[at][at]
    shift_by = DAMPING * traced / 6.0
    for at in range(6):
        entries[at][at] = entries[at][at] + shift_by
    values = [-rows[AT_AM + i] for i in range(3)] + [-rows[AT_NM + i] for i in range(3)]
    for pivot in range(6):
        for row in range(pivot + 1, 6):
            factor = entries[row][pivot] / entries[pivot][pivot]
            for col in range(pivot + 1, 6):
                entries[row][col] = entries[row][col] - factor * entries[pivot][col]
            values[row] = values[row] - factor * values[pivot]
    result = [None] * 6
    for row in range(5, -1, -1):
        running = values[row]
        for col in range(row + 1, 6):
            running = running - entries[row][col] * result[col]
        result[row] = running / entries[row][row]
    return result


def cross(u, v):
    return [u[1] * v[2] - u[2] * v[1], u[2] * v[0] - u[0] * v[2], u[0] * v[1] - u[1] * v[0]]


def kernel(
    dest_hbm, scan_hbm, src_hbm, mat_hbm, tp_hbm, tn_hbm, out_ref,
    dest_v, scan_s, src_v, mat_v, tp_v, tn_v, inv_v, inv_s, table, rhs,
    send, recv, ucat, sums, ret_send, ret_recv, total, total_far,
    in_sem, inv_sem, send_sem, recv_sem, ret_ssem, ret_rsem, far_ssem, far_rsem,
):
    me_grp, me = lax.axis_index("grp"), lax.axis_index("tile")
    z, y, x = me // 16, (me // 4) % 4, me % 4

    barrier = pltpu.get_barrier_semaphore()

    def announce(at, carry):
        pl.semaphore_signal(barrier, 1, device_id={"tile": (me + at) % TILES})
        return carry

    pl.semaphore_signal(barrier, 1, device_id={"grp": 1 - me_grp})
    lax.fori_loop(1, TILES, announce, 0)

    copies = [
        pltpu.make_async_copy(s, d, in_sem.at[i])
        for i, (s, d) in enumerate(
            [(dest_hbm, dest_v), (scan_hbm, scan_s), (src_hbm, src_v), (mat_hbm, mat_v), (tp_hbm, tp_v), (tn_hbm, tn_v)]
        )
    ]
    for copy in copies:
        copy.start()

    copies[0].wait()
    blocks = jnp.broadcast_to(dest_v[...], (LANES, LANES)).T
    lane = lax.broadcasted_iota(I32, (LANES, LANES), 1)
    number = lax.broadcasted_iota(I32, (LANES, LANES), 0)
    named = blocks == lane
    first = jnp.min(jnp.where(named, number, 1000), axis=0, keepdims=True)
    last = jnp.max(jnp.where(named, number, -1), axis=0, keepdims=True)
    first = jnp.where(last < 0, -1, first)
    last = jnp.where(last == first, -1, last)
    inv_v[...] = jnp.concatenate([first, last], axis=0)
    to_smem = pltpu.make_async_copy(inv_v, inv_s, inv_sem)
    to_smem.start()
    for copy in copies[1:4]:
        copy.wait()
    to_smem.wait()

    def pack(d, carry):
        slots = send.at[pl.ds(pl.multiple_of(d * 16, 16), 16)]
        for r in range(2):
            l = inv_s[r, d]
            held = jnp.minimum(jnp.maximum(l, 0), TILES - 1)
            scale = jnp.where(l >= 0, 1, 0)
            base = jnp.where(l >= 0, scan_s[0, held] * TARGET_PTS, -1)
            for c in range(3):
                slots[r * 8 + 2 * c : r * 8 + 2 * c + 2, :] = src_v[c * TILES + held]
            slots[r * 8 + 6 : r * 8 + 8, :] = (mat_v[held] * scale + base).astype(F32)
        return carry

    lax.fori_loop(0, TILES, pack, 0, unroll=4)
    pl.semaphore_wait(barrier, TILES)

    def offset_of(group):
        return group % 4, group // 4

    def out_copy(group, j, dz):
        dx, dy = offset_of(group)
        to = ((z + dz) % 8) * 16 + ((y + dy) % 4) * 4 + (x + dx) % 4
        k = group * 8 + j
        return pltpu.make_async_remote_copy(
            src_ref=send.at[pl.ds(pl.multiple_of(to * 16, 16), 16)],
            dst_ref=recv.at[pl.ds(pl.multiple_of(k * 16, 16), 16)],
            send_sem=send_sem,
            recv_sem=recv_sem.at[group],
            device_id={"tile": to},
        )

    def issue(step, carry):
        group = 15 - step
        for j, dz in enumerate(DZ_ORDER):
            out_copy(group, j, dz).start()
        return carry

    lax.fori_loop(0, 15, issue, 0)
    for j, dz in enumerate(DZ_ORDER[:-1]):
        out_copy(0, j, dz).start()
    recv[7 * 16 : 8 * 16, :] = send[pl.ds(pl.multiple_of(me * 16, 16), 16), :]

    copies[4].wait()
    copies[5].wait()

    def spread(at, carry):
        rows = table.at[pl.ds(pl.multiple_of(at * 8, 8), 8)]
        columns = pl.ds(pl.multiple_of(at * LANES, LANES), LANES)
        rows[0:3, :] = tp_v[:, columns]
        rows[3:6, :] = tn_v[:, columns]
        return carry

    lax.fori_loop(0, 4 * SCANS_DEV, spread, 0, unroll=8)
    for c in range(6):
        for chunk in range(4):
            column = jnp.concatenate(
                [table[pl.ds((s8 * 32 + chunk) * 8 + c, 8, stride=32), :] for s8 in range(8)], axis=0
            )
            at = (c * 4 + chunk) * LANES
            for part, piece in enumerate(parts_of(column)):
                rhs[part * 64 : (part + 1) * 64, at : at + LANES] = piece

    lane8 = lax.broadcasted_iota(I32, (8, LANES), 1)

    def settle(group):
        base = group * LANES
        wanted = [
            [recv[pl.ds(base + r * 8 + 6 + h, 8, stride=16), :].astype(I32) for h in range(2)] for r in range(2)
        ]
        points = [
            [[recv[pl.ds(base + r * 8 + 2 * c + h, 8, stride=16), :] for c in range(3)] for h in range(2)]
            for r in range(2)
        ]
        scan = [lax.shift_right_arithmetic(wanted[r][0][:, 0:1], 9) for r in range(2)]
        column = lax.broadcasted_iota(I32, (8, 3 * SCANS_DEV), 1) & (SCANS_DEV - 1)
        picks = jnp.concatenate([jnp.where(column == scan[r], 1.0, 0.0) for r in range(2)], axis=0)
        picks = picks.astype(jnp.bfloat16)
        inside = [[wanted[r][h] & (LANES - 1) for h in range(2)] for r in range(2)]
        odd = [[(wanted[r][h] & LANES) != 0 for h in range(2)] for r in range(2)]
        upper = [[(wanted[r][h] & (2 * LANES)) != 0 for h in range(2)] for r in range(2)]
        found = [[[None] * 6 for _ in range(2)] for _ in range(2)]
        for c in range(6):
            held = jnp.dot(picks, rhs[:, c * TARGET_PTS : (c + 1) * TARGET_PTS], preferred_element_type=F32)
            for r in range(2):
                chunk = [held[r * 8 : r * 8 + 8, q * LANES : (q + 1) * LANES] for q in range(4)]
                for h in range(2):
                    got = [jnp.take_along_axis(chunk[q], inside[r][h], axis=1, mode="promise_in_bounds") for q in range(4)]
                    found[r][h][c] = jnp.where(
                        upper[r][h],
                        jnp.where(odd[r][h], got[3], got[2]),
                        jnp.where(odd[r][h], got[1], got[0]),
                    )
        result = jnp.zeros((8, LANES), F32)
        for r in range(2):
            terms = []
            for h in range(2):
                p, q, n = points[r][h], found[r][h][:3], found[r][h][3:]
                a, b = cross(p, n), cross(q, n)
                m = n[0] * (p[0] - q[0]) + n[1] * (p[1] - q[1]) + n[2] * (p[2] - q[2])
                terms.append((a, b, n, m))

            def summed(left, right):
                return jnp.sum(left(0) * right(0) + left(1) * right(1), axis=1, keepdims=True)

            def pick(which, i):
                return lambda h: terms[h][which] if i is None else terms[h][which][i]

            places = []
            for at, (i, j) in enumerate(PAIRS):
                places.append((at, pick(0, i), pick(0, j), 1))
                places.append((AT_NN + at, pick(2, i), pick(2, j), 1))
                places.append((AT_B + at, pick(1, i), pick(1, j), 1))
            for i in range(3):
                for j in range(3):
                    places.append((AT_AN + 3 * i + j, pick(0, i), pick(2, j), 1))
                    places.append((AT_B + AT_AN + 3 * i + j, pick(1, i), pick(2, j), 1))
                places.append((AT_AM + i, pick(0, i), pick(3, None), 1))
                places.append((AT_NM + i, pick(2, i), pick(3, None), 1))
                places.append((AT_B + AT_AM + i, pick(1, i), pick(3, None), -1))
            for at, left, right, sign in places:
                value = summed(left, right)
                result = jnp.where(lane8 == at + 64 * r, value if sign > 0 else -value, result)
        which = jnp.where(lane8 < 64, scan[0], scan[1])
        rows = pl.ds(pl.multiple_of(group * 8, 8), 8)
        ucat[rows, :] = jnp.where((lane8 & 63) == which, 1.0, 0.0)
        sums[rows, :] = result
        for i in range(8):
            ret_send[group * 8 + i] = result[i : i + 1, :]

    def back_copy(group, j, dz):
        dx, dy = offset_of(group)
        to = ((z + 8 - dz) % 8) * 16 + ((y + 4 - dy) % 4) * 4 + (x + 4 - dx) % 4
        return pltpu.make_async_remote_copy(
            src_ref=ret_send.at[group * 8 + j],
            dst_ref=ret_recv.at[me],
            send_sem=ret_ssem,
            recv_sem=ret_rsem,
            device_id={"tile": to},
        )

    def landed(first_row, rows, sem):
        return pltpu.make_async_copy(recv.at[pl.ds(first_row, rows)], recv.at[pl.ds(first_row, rows)], sem)

    def work(step, carry):
        group = 15 - step
        landed(pl.multiple_of(group * LANES, LANES), LANES, recv_sem.at[group]).wait()
        settle(group)
        for j, dz in enumerate(DZ_ORDER):
            back_copy(group, j, dz).start()
        return carry

    lax.fori_loop(0, 15, work, 0)
    landed(0, 7 * 16, recv_sem.at[0]).wait()
    settle(0)
    for j, dz in enumerate(DZ_ORDER[:-1]):
        back_copy(0, j, dz).start()
    ret_recv[me] = ret_send[7]

    by_target = jnp.dot(ucat[...].T, sums[...], precision=PRECISE, preferred_element_type=F32)
    by_target = by_target[:64] + pltpu.roll(by_target[64:], 64, axis=1)
    lane64 = lax.broadcasted_iota(I32, (SCANS_DEV, LANES), 1)
    moved = pltpu.roll(by_target, LANES - AT_B, axis=1)
    by_target = jnp.where(
        lane64 < AT_NN, moved, jnp.where(lane64 < AT_NM, by_target, jnp.where(lane64 < AT_NM + 3, -by_target, 0.0))
    )
    scan_row = lax.broadcasted_iota(I32, (SCANS_DEV, LANES), 0)
    owner = [lax.shift_right_arithmetic(inv_v[r : r + 1, :], 1) for r in range(2)]
    scat = jnp.concatenate([jnp.where(scan_row == owner[r], 1.0, 0.0) for r in range(2)], axis=0)

    others = ret_recv.at[pl.ds(0, TILES - 1)]
    pltpu.make_async_copy(others, others, ret_rsem).wait()
    returned = ret_recv[...].reshape(TILES, LANES)
    by_source = jnp.dot(scat, returned, precision=PRECISE, preferred_element_type=F32)
    by_source = by_source[:64] + pltpu.roll(by_source[64:], 64, axis=1)
    both = by_source + by_target
    flipped = jnp.concatenate([both, jnp.zeros_like(both)], axis=0).T
    total[...] = flipped[:32, :]
    far = pltpu.make_async_remote_copy(
        src_ref=total, dst_ref=total_far, send_sem=far_ssem, recv_sem=far_rsem, device_id={"grp": 1 - me_grp}
    )
    far.start()
    far.wait_recv()
    whole = total[...] + total_far[...]
    result = solve_rows([whole[at : at + 1, :] for at in range(27)])
    for row in range(6):
        out_ref[row : row + 1, :] = result[row][:, :SCANS_DEV]
    far.wait_send()
    ret_others = ret_send.at[pl.ds(0, TILES - 1)]
    pltpu.make_async_copy(ret_others, ret_others, ret_ssem).wait()
    sent = send.at[pl.ds(0, 16 * (TILES - 1))]
    pltpu.make_async_copy(sent, sent, send_sem).wait()


def body(source_points, intersection, target_scan, matches, target_points, target_normals):
    anywhere = pl.BlockSpec(memory_space=pl.ANY)
    vmem = pltpu.VMEM
    dma = pltpu.SemaphoreType.DMA
    return pl.pallas_call(
        kernel,
        name="icp_step",
        out_shape=jax.ShapeDtypeStruct((6, SCANS_DEV), F32),
        in_specs=[anywhere] * 6,
        out_specs=pl.BlockSpec(memory_space=pltpu.VMEM),
        scratch_shapes=[
            vmem((1, TILES), I32),
            pltpu.SMEM((1, TILES), I32),
            vmem((3 * TILES, 2, LANES), F32),
            vmem((TILES, 2, LANES), I32),
            vmem((3, SCANS_DEV * TARGET_PTS), F32),
            vmem((3, SCANS_DEV * TARGET_PTS), F32),
            vmem((2, TILES), I32),
            pltpu.SMEM((2, TILES), I32),
            vmem((SCANS_DEV * 4 * 8 + 32, LANES), F32),
            vmem((3 * SCANS_DEV, 6 * TARGET_PTS), jnp.bfloat16),
            vmem((TILES * 16, LANES), F32),
            vmem((TILES * 16 + 16, LANES), F32),
            vmem((TILES, LANES), F32),
            vmem((TILES, LANES), F32),
            vmem((TILES, 1, LANES), F32),
            vmem((TILES, 1, LANES), F32),
            vmem((32, LANES), F32),
            vmem((32, LANES), F32),
            dma((6,)),
            dma,
            dma,
            dma((16,)),
            dma,
            dma,
            dma,
            dma,
        ],
        compiler_params=pltpu.CompilerParams(collective_id=0, has_side_effects=True),
    )(
        intersection.reshape(1, TILES),
        target_scan,
        source_points.reshape(3 * TILES, 2, LANES),
        matches.reshape(TILES, 2, LANES),
        target_points,
        target_normals,
    )


def solution(mesh):
    in_specs = (
        P("grp", None, "tile"),
        P("grp", "tile", None),
        P("grp", "tile"),
        P("grp", "tile"),
        P(None, "tile"),
        P(None, "tile"),
    )
    return jax.shard_map(body, mesh=mesh, in_specs=in_specs, out_specs=P(None, "tile"), check_vma=False)
```

time: 200 us -> 48.8 us (0.24)
  matrix products: 71.8 us -> 0 us
  Pallas kernels: 0 us -> 47.4 us
  local copies, waits for them, and re-layouts: 43.1 us -> 1.28 us
  waiting for transfers between devices: 37.4 us -> 0 us
  starting transfers between devices: 24.3 us -> 0 us
  other arithmetic: 17.8 us -> 0 us
  blocking collectives: 4.25 us -> 0 us
    dot_general x25 -> x0, matrix products: 71.8 us -> none  [the longest x16 54.5 us: select(): return jnp.einsum('icj,ijk->ick', table_part, chooser, precision=PRECISE)]
    pallas_call x0 -> x1, Pallas kernels: none -> 47.4 us  [body(): pl.pallas_call(kernel, name='icp_step', out_shape=jax.ShapeDtypeStruct((6...]
    all_to_all x2 -> x0, waiting for transfers between devices: 37.4 us -> none  [the longest x1 28.5 us: body(): lax.all_to_all(outgoing, 'tile', split_axis=1, concat_axis=1, tiled=True)]
    all_to_all x2 -> x0, starting transfers between devices: 24.3 us -> none  [the longest x1 16.3 us: body(): lax.all_to_all(outgoing, 'tile', split_axis=1, concat_axis=1, tiled=True)]
    dynamic_slice x16 -> x0, local copies, waits for them, and re-layouts: 15 us -> none  [body(): lax.map(select, (block_tables.reshape(items // group, group, 6, TARGET_PT...]
    slice x13 -> x0, local copies, waits for them, and re-layouts: 10.5 us -> none  [the longest x2 3 us: pair_terms(): normal_blocks[6:, 6:].reshape((36,) + layout)]
    squeeze x7 -> x0, local copies, waits for them, and re-layouts: 9.17 us -> none  [the longest x1 1.92 us: cross_rows(): first_vec[2] * second_vec[1]]
    unnamed x5 -> x0, other arithmetic: 8.4 us -> none
  transfers between devices with their start and end apart: 2 -> 0, of which waited for: 2 -> 0; matrix products, arithmetic and copies ran while one was open for 1% -> 0% of each run, Pallas kernels for 0% -> 0%
where the time goes in v1:
time: 48.8 us; the launch traced here: 48.7 us
  Pallas kernels  47.4 us (97%)
  local copies, waits for them, and re-layouts  1.28 us (3%)
    pallas_call x1, Pallas kernels, body(): pl.pallas_call(kernel, name='icp_step', out_shape=jax.ShapeDtypeStruct((6...  47.4 us
    unnamed x1, local copies, waits for them, and re-layouts  1.28 us

profile of v1, /device:TPU:1, one launch (start us, length us, event | category | flops | bytes accessed | tf_op | source)
XLA Modules:
  0.0 48.7 jit_solution(2912520459024556370)
XLA Ops:
  0.0 47.4 %icp_step.1 = f32[6,64]{1,0:T(8,128)} custom-call(s32[1,128]{1,0:T(1,128)} %bitcast.5, s32[1,128]{1,0:T(1,128)} %scan_hbm.1, f32[384,2,128]{2,1,0:T(2,128)} %bitcast.3, s32[128,2,128]{2,1,0:T(2,128)} %bitcast.4, f32[3,32768]{1,0:T(4,128)} %tp_hbm.1, f32[3,32768]{1,0:T(4,128)} %tn_hbm.1), custom_call_target="tpu_custom_call" | custom-call | tf_op jit(solution)/shard_map/icp_step/pallas_call | solution.py:303
  47.4 1.3 %copy.8 = f32[6,64]{1,0:T(8,128)} copy(f32[6,64]{1,0:T(8,128)} %icp_step.1) | data formatting | bytes 3072

commit v2 on v1

v2 whole, which is shorter than its diff:
```python
import jax
import jax.numpy as jnp
from jax import lax
from jax.experimental import pallas as pl
from jax.experimental.pallas import tpu as pltpu
from jax.sharding import PartitionSpec as P

TILES = 128
SCANS_DEV = 64
TARGET_PTS = 512
LANES = 128
DAMPING = 0.1
PRECISE = lax.Precision.HIGHEST
F32 = jnp.float32
I32 = jnp.int32
DZ_ORDER = (4, 3, 5, 2, 6, 1, 7, 0)
PLANE = 16
LAG = 5
LEAD = 4

PAIRS = [(i, j) for i in range(3) for j in range(i, 3)]
AT_AN, AT_AM, AT_NN, AT_NM, AT_B = 6, 15, 18, 24, 32


def parts_of(value):
    high = value.astype(jnp.bfloat16)
    rest = value - high.astype(F32)
    middle = rest.astype(jnp.bfloat16)
    low = (rest - middle.astype(F32)).astype(jnp.bfloat16)
    return high, middle, low


def solve_rows(rows):
    entries = [[None] * 6 for _ in range(6)]
    for at, (i, j) in enumerate(PAIRS):
        entries[i][j] = entries[j][i] = rows[at]
        entries[3 + i][3 + j] = entries[3 + j][3 + i] = rows[AT_NN + at]
    for i in range(3):
        for j in range(3):
            entries[i][3 + j] = entries[3 + j][i] = rows[AT_AN + 3 * i + j]
    traced = entries[0][0]
    for at in range(1, 6):
        traced = traced + entries[at][at]
    shift_by = DAMPING * traced / 6.0
    for at in range(6):
        entries[at][at] = entries[at][at] + shift_by
    values = [-rows[AT_AM + i] for i in range(3)] + [-rows[AT_NM + i] for i in range(3)]
    for pivot in range(6):
        for row in range(pivot + 1, 6):
            factor = entries[row][pivot] / entries[pivot][pivot]
            for col in range(pivot + 1, 6):
                entries[row][col] = entries[row][col] - factor * entries[pivot][col]
            values[row] = values[row] - factor * values[pivot]
    result = [None] * 6
    for row in range(5, -1, -1):
        running = values[row]
        for col in range(row + 1, 6):
            running = running - entries[row][col] * result[col]
        result[row] = running / entries[row][row]
    return result


def cross(u, v):
    return [u[1] * v[2] - u[2] * v[1], u[2] * v[0] - u[0] * v[2], u[0] * v[1] - u[1] * v[0]]


def turn(at):
    return (2 + 3 * at + 3 * ((at * (at - 1)) // 2)) % 4


def kernel(
    dest_hbm, scan_hbm, src_hbm, mat_hbm, tp_hbm, tn_hbm, out_ref,
    dest_v, scan_s, src_v, mat_v, tp_v, tn_v, inv_v, inv_s, table, rhs, held,
    send, relay, recv, ucat, sums, ret_send, ret_recv, total, total_far,
    in_sem, inv_sem, send_sem, relay_sem, onward_sem, recv_sem,
    ret_ssem, ret_rsem, far_ssem, far_rsem,
):
    me_grp, me = lax.axis_index("grp"), lax.axis_index("tile")
    z, y, x = me // PLANE, (me // 4) % 4, me % 4
    level = me - me % PLANE
    spot = me % PLANE

    def in_plane(group, sign):
        dx, dy = turn(group % 4), turn(group // 4)
        return level + ((y + 4 + sign * dy) % 4) * 4 + (x + 4 + sign * dx) % 4

    def along_z(dz):
        return ((z + dz) % 8) * PLANE + spot

    copies = [
        pltpu.make_async_copy(s, d, in_sem.at[i])
        for i, (s, d) in enumerate(
            [(dest_hbm, dest_v), (scan_hbm, scan_s), (src_hbm, src_v), (mat_hbm, mat_v), (tp_hbm, tp_v), (tn_hbm, tn_v)]
        )
    ]
    for copy in copies:
        copy.start()

    barrier = pltpu.get_barrier_semaphore()
    for dz in DZ_ORDER[:-1]:
        pl.semaphore_signal(barrier, 1, device_id={"tile": along_z(dz)})

    def announce(group, carry):
        pl.semaphore_signal(barrier, 1, device_id={"tile": in_plane(group, 1)})
        return carry

    lax.fori_loop(0, 15, announce, 0, unroll=5)
    pl.semaphore_signal(barrier, 1, device_id={"grp": 1 - me_grp})

    copies[0].wait()
    blocks = jnp.broadcast_to(dest_v[...], (LANES, LANES)).T
    lane = lax.broadcasted_iota(I32, (LANES, LANES), 1)
    number = lax.broadcasted_iota(I32, (LANES, LANES), 0)
    named = blocks == lane
    first = jnp.min(jnp.where(named, number, 1000), axis=0, keepdims=True)
    last = jnp.max(jnp.where(named, number, -1), axis=0, keepdims=True)
    first = jnp.where(last < 0, -1, first)
    last = jnp.where(last == first, -1, last)
    inv_v[...] = jnp.concatenate([first, last], axis=0)
    to_smem = pltpu.make_async_copy(inv_v, inv_s, inv_sem)
    to_smem.start()
    for copy in copies[1:4]:
        copy.wait()
    to_smem.wait()

    def pack(group, carry):
        place = in_plane(group, 1) % PLANE
        for j, dz in enumerate(DZ_ORDER):
            d = ((z + dz) % 8) * PLANE + place
            slots = send.at[pl.ds(pl.multiple_of(group * LANES, LANES) + j * 16, 16)]
            for r in range(2):
                l = inv_s[r, d]
                block = jnp.minimum(jnp.maximum(l, 0), TILES - 1)
                scale = jnp.where(l >= 0, 1, 0)
                base = jnp.where(l >= 0, scan_s[0, block] * TARGET_PTS, -1)
                for c in range(3):
                    slots[r * 8 + 2 * c : r * 8 + 2 * c + 2, :] = src_v[c * TILES + block]
                slots[r * 8 + 6 : r * 8 + 8, :] = (mat_v[block] * scale + base).astype(F32)
        return carry

    lax.fori_loop(0, LEAD, pack, 0, unroll=2)
    pl.semaphore_wait(barrier, 7 + 15 + 1)

    def rows_of(group, j=0, count=8):
        return pl.ds(pl.multiple_of(group * LANES, LANES) + j * 16, count * 16)

    def z_copy(source, target, group, j, sent, sem):
        return pltpu.make_async_remote_copy(
            src_ref=source.at[rows_of(group, j, 1)],
            dst_ref=target.at[rows_of(group, j, 1)],
            send_sem=sent,
            recv_sem=sem.at[group],
            device_id={"tile": along_z(DZ_ORDER[j])},
        )

    def plane_copy(source, target, group, sent, sem):
        return pltpu.make_async_remote_copy(
            src_ref=source.at[rows_of(group)],
            dst_ref=target.at[rows_of(group)],
            send_sem=sent,
            recv_sem=sem.at[group],
            device_id={"tile": in_plane(group, 1)},
        )

    def landed(ref, group, sem, count=8):
        piece = ref.at[rows_of(group, 0, count)]
        return pltpu.make_async_copy(piece, piece, sem.at[group])

    def issue(group, carry):
        for j in range(7):
            z_copy(send, relay, group, j, send_sem, relay_sem).start()
        relay[rows_of(group, 7, 1), :] = send[rows_of(group, 7, 1), :]
        return carry

    def issue_plane(group, carry):
        plane_copy(send, relay, group, send_sem, relay_sem).start()
        return carry

    lax.fori_loop(0, LEAD, issue, 0)
    lax.fori_loop(8, 16, pack, 0, unroll=2)
    lax.fori_loop(8, 15, issue_plane, 0)
    lax.fori_loop(LEAD, 8, pack, 0, unroll=2)

    copies[4].wait()
    copies[5].wait()

    def spread(at, carry):
        rows = table.at[pl.ds(pl.multiple_of(at * 8, 8), 8)]
        columns = pl.ds(pl.multiple_of(at * LANES, LANES), LANES)
        rows[0:3, :] = tp_v[:, columns]
        rows[3:6, :] = tn_v[:, columns]
        return carry

    lax.fori_loop(0, 4 * SCANS_DEV, spread, 0, unroll=8)
    for c in range(6):
        for chunk in range(4):
            column = jnp.concatenate(
                [table[pl.ds((s8 * 32 + chunk) * 8 + c, 8, stride=32), :] for s8 in range(8)], axis=0
            )
            at = (c * 4 + chunk) * LANES
            for part, piece in enumerate(parts_of(column)):
                rhs[part * 64 : (part + 1) * 64, at : at + LANES] = piece

    lane8 = lax.broadcasted_iota(I32, (8, LANES), 1)

    def settle(groups):
        batches = [(g, r) for g in range(len(groups)) for r in range(2)]

        def rows(g, r, row):
            return recv[pl.ds(groups[g] * LANES + r * 8 + row, 8, stride=16), :]

        wanted = {(g, r, h): rows(g, r, 6 + h).astype(I32) for g, r in batches for h in range(2)}
        scan = {(g, r): lax.shift_right_arithmetic(wanted[g, r, 0][:, 0:1], 9) for g, r in batches}
        column = lax.broadcasted_iota(I32, (8, 3 * SCANS_DEV), 1) & (SCANS_DEV - 1)
        picks = jnp.concatenate([jnp.where(column == scan[b], 1.0, 0.0) for b in batches], axis=0)
        held[: picks.shape[0], :] = jnp.dot(picks.astype(jnp.bfloat16), rhs[...], preferred_element_type=F32)
        for g in range(len(groups)):
            result = jnp.zeros((8, LANES), F32)
            for r in range(2):
                terms = []
                for h in range(2):
                    inside = wanted[g, r, h] & (LANES - 1)
                    odd = (wanted[g, r, h] & LANES) != 0
                    upper = (wanted[g, r, h] & (2 * LANES)) != 0
                    found = []
                    for c in range(6):
                        got = [
                            jnp.take_along_axis(
                                held[(2 * g + r) * 8 : (2 * g + r) * 8 + 8, (4 * c + q) * LANES : (4 * c + q + 1) * LANES],
                                inside, axis=1, mode="promise_in_bounds",
                            )
                            for q in range(4)
                        ]
                        found.append(jnp.where(upper, jnp.where(odd, got[3], got[2]), jnp.where(odd, got[1], got[0])))
                    p, q, n = [rows(g, r, 2 * c + h) for c in range(3)], found[:3], found[3:]
                    a, b = cross(p, n), cross(q, n)
                    m = n[0] * (p[0] - q[0]) + n[1] * (p[1] - q[1]) + n[2] * (p[2] - q[2])
                    terms.append((a, b, n, [m]))

                def put(result, at, left, i, right, j, sign=1):
                    total = terms[0][left][i] * terms[0][right][j] + terms[1][left][i] * terms[1][right][j]
                    value = jnp.sum(total, axis=1, keepdims=True)
                    return jnp.where(lane8 == at + 64 * r, value if sign > 0 else -value, result)

                for at, (i, j) in enumerate(PAIRS):
                    result = put(result, at, 0, i, 0, j)
                    result = put(result, AT_NN + at, 2, i, 2, j)
                    result = put(result, AT_B + at, 1, i, 1, j)
                for i in range(3):
                    for j in range(3):
                        result = put(result, AT_AN + 3 * i + j, 0, i, 2, j)
                        result = put(result, AT_B + AT_AN + 3 * i + j, 1, i, 2, j)
                    result = put(result, AT_AM + i, 0, i, 3, 0)
                    result = put(result, AT_NM + i, 2, i, 3, 0)
                    result = put(result, AT_B + AT_AM + i, 1, i, 3, 0, -1)
            which = jnp.where(lane8 < 64, scan[g, 0], scan[g, 1])
            block = pl.ds(pl.multiple_of(groups[g] * 8, 8), 8)
            ucat[block, :] = jnp.where((lane8 & 63) == which, 1.0, 0.0)
            sums[block, :] = result
            for i in range(8):
                ret_send[groups[g] * 8 + i] = result[i : i + 1, :]

    def back_copy(group, j):
        to = ((z + 8 - DZ_ORDER[j]) % 8) * PLANE + in_plane(group, -1) % PLANE
        return pltpu.make_async_remote_copy(
            src_ref=ret_send.at[group * 8 + j],
            dst_ref=ret_recv.at[me],
            send_sem=ret_ssem,
            recv_sem=ret_rsem,
            device_id={"tile": to},
        )

    def give_back(group, count=8):
        for j in range(count):
            back_copy(group, j).start()

    def onward(step):
        landed(relay, step, relay_sem, 7).wait()
        plane_copy(relay, recv, step, onward_sem, recv_sem).start()

    def onward_z(group):
        landed(relay, group, relay_sem).wait()
        for j in range(7):
            z_copy(relay, recv, group, j, onward_sem, recv_sem).start()
        recv[rows_of(group, 7, 1), :] = relay[rows_of(group, 7, 1), :]

    def work(pair):
        landed(recv, pair, recv_sem).wait()
        landed(recv, pair + 8, recv_sem, 7).wait()
        settle([pair, pair + 8])
        give_back(pair)
        give_back(pair + 8)

    def early(step, carry):
        onward(step)
        onward_z(step + 8)

        @pl.when(step + LEAD < 8)
        def _():
            issue(step + LEAD, 0)

        return carry

    def early_and_work(step, carry):
        early(step, carry)
        work(step - LAG)
        return carry

    def late(pair, carry):
        work(pair)
        return carry

    lax.fori_loop(0, LAG, early, 0)
    lax.fori_loop(LAG, 7, early_and_work, 0)
    onward(7)
    for j in range(7):
        z_copy(send, recv, 15, j, send_sem, recv_sem).start()
    recv[rows_of(15, 7, 1), :] = send[rows_of(15, 7, 1), :]
    lax.fori_loop(7 - LAG, 6, late, 0)
    landed(recv, 7, recv_sem).wait()
    settle([7])
    give_back(7)
    lax.fori_loop(6, 7, late, 0)
    landed(recv, 15, recv_sem, 7).wait()
    settle([15])
    give_back(15, 7)
    ret_recv[me] = ret_send[15 * 8 + 7]

    by_target = jnp.dot(ucat[...].T, sums[...], precision=PRECISE, preferred_element_type=F32)
    by_target = by_target[:64] + pltpu.roll(by_target[64:], 64, axis=1)
    lane64 = lax.broadcasted_iota(I32, (SCANS_DEV, LANES), 1)
    moved = pltpu.roll(by_target, LANES - AT_B, axis=1)
    by_target = jnp.where(
        lane64 < AT_NN, moved, jnp.where(lane64 < AT_NM, by_target, jnp.where(lane64 < AT_NM + 3, -by_target, 0.0))
    )
    scan_row = lax.broadcasted_iota(I32, (SCANS_DEV, LANES), 0)
    owner = [lax.shift_right_arithmetic(inv_v[r : r + 1, :], 1) for r in range(2)]
    scat = jnp.concatenate([jnp.where(scan_row == owner[r], 1.0, 0.0) for r in range(2)], axis=0)

    sent = send.at[pl.ds(0, 8 * 7 * 16 + 7 * 8 * 16 + 7 * 16)]
    pltpu.make_async_copy(sent, sent, send_sem).wait()
    moved_on = relay.at[pl.ds(0, 8 * 8 * 16 + 7 * 7 * 16)]
    pltpu.make_async_copy(moved_on, moved_on, onward_sem).wait()
    others = ret_recv.at[pl.ds(0, TILES - 1)]
    pltpu.make_async_copy(others, others, ret_rsem).wait()
    gone = ret_send.at[pl.ds(0, TILES - 1)]
    pltpu.make_async_copy(gone, gone, ret_ssem).wait()
    returned = ret_recv[...].reshape(TILES, LANES)
    by_source = jnp.dot(scat, returned, precision=PRECISE, preferred_element_type=F32)
    by_source = by_source[:64] + pltpu.roll(by_source[64:], 64, axis=1)
    both = by_source + by_target
    flipped = jnp.concatenate([both, jnp.zeros_like(both)], axis=0).T
    total[...] = flipped[:32, :]
    far = pltpu.make_async_remote_copy(
        src_ref=total, dst_ref=total_far, send_sem=far_ssem, recv_sem=far_rsem, device_id={"grp": 1 - me_grp}
    )
    far.start()
    far.wait_recv()
    whole = total[...] + total_far[...]
    result = solve_rows([whole[at : at + 1, :] for at in range(27)])
    for row in range(6):
        out_ref[row : row + 1, :] = result[row]
    far.wait_send()


def body(source_points, intersection, target_scan, matches, target_points, target_normals):
    anywhere = pl.BlockSpec(memory_space=pl.ANY)
    vmem = pltpu.VMEM
    dma = pltpu.SemaphoreType.DMA
    steps = pl.pallas_call(
        kernel,
        name="icp_step",
        out_shape=jax.ShapeDtypeStruct((8, LANES), F32),
        in_specs=[anywhere] * 6,
        out_specs=pl.BlockSpec(memory_space=pltpu.VMEM),
        scratch_shapes=[
            vmem((1, TILES), I32),
            pltpu.SMEM((1, TILES), I32),
            vmem((3 * TILES, 2, LANES), F32),
            vmem((TILES, 2, LANES), I32),
            vmem((3, SCANS_DEV * TARGET_PTS), F32),
            vmem((3, SCANS_DEV * TARGET_PTS), F32),
            vmem((2, TILES), I32),
            pltpu.SMEM((2, TILES), I32),
            vmem((SCANS_DEV * 4 * 8 + 32, LANES), F32),
            vmem((3 * SCANS_DEV, 6 * TARGET_PTS), jnp.bfloat16),
            vmem((32, 6 * TARGET_PTS), F32),
            vmem((TILES * 16, LANES), F32),
            vmem((TILES * 16, LANES), F32),
            vmem((TILES * 16 + 16, LANES), F32),
            vmem((TILES, LANES), F32),
            vmem((TILES, LANES), F32),
            vmem((TILES, 1, LANES), F32),
            vmem((TILES, 1, LANES), F32),
            vmem((32, LANES), F32),
            vmem((32, LANES), F32),
            dma((6,)),
            dma,
            dma,
            dma((16,)),
            dma,
            dma((16,)),
            dma,
            dma,
            dma,
            dma,
        ],
        compiler_params=pltpu.CompilerParams(collective_id=0, has_side_effects=True),
    )(
        intersection.reshape(1, TILES),
        target_scan,
        source_points.reshape(3 * TILES, 2, LANES),
        matches.reshape(TILES, 2, LANES),
        target_points,
        target_normals,
    )
    return steps[:6, :SCANS_DEV]


def solution(mesh):
    in_specs = (
        P("grp", None, "tile"),
        P("grp", "tile", None),
        P("grp", "tile"),
        P("grp", "tile"),
        P(None, "tile"),
        P(None, "tile"),
    )
    return jax.shard_map(body, mesh=mesh, in_specs=in_specs, out_specs=P(None, "tile"), check_vma=False)
```

time: 48.8 us -> 47.3 us (0.969)
  Pallas kernels: 47.4 us -> 45.9 us
    pallas_call x1, Pallas kernels: 47.4 us -> 45.9 us  [body(): pl.pallas_call(kernel, name='icp_step', out_shape=jax.ShapeDtypeStruct((8...]
where the time goes in v2:
time: 47.3 us; the launch traced here: 47.2 us
  Pallas kernels  45.9 us (97%)
  local copies, waits for them, and re-layouts  1.28 us (3%)
    pallas_call x1, Pallas kernels, body(): pl.pallas_call(kernel, name='icp_step', out_shape=jax.ShapeDtypeStruct((8...  45.9 us
    unnamed x1, local copies, waits for them, and re-layouts  1.28 us

profile of v2, /device:TPU:1, one launch (start us, length us, event | category | flops | bytes accessed | tf_op | source)
XLA Modules:
  0.0 47.2 jit_solution(3366680248349509893)
XLA Ops:
  0.0 45.9 %icp_step.1 = f32[8,128]{1,0:T(8,128)} custom-call(s32[1,128]{1,0:T(1,128)} %bitcast.7, s32[1,128]{1,0:T(1,128)} %scan_hbm.1, f32[384,2,128]{2,1,0:T(2,128)} %bitcast.4, s32[128,2,128]{2,1,0:T(2,128)} %bitcast.5, f32[3,32768]{1,0:T(4,128)} %tp_hbm.1, f32[3,32768]{1,0:T(4,128)} %tn_hbm.1), custom_call_target="tpu_custom_call" | custom-call | tf_op jit(solution)/shard_map/icp_step/pallas_call | solution.py:370
  45.9 1.3 %copy.8 = f32[6,64]{1,0:T(8,128)} copy(f32[6,64]{1,0:T(8,128)} %bitcast.6) | data formatting | bytes 3072

commit v3 on v2

--- a/solution.py
+++ b/solution.py
@@ -15,8 +15,6 @@
 I32 = jnp.int32
 DZ_ORDER = (4, 3, 5, 2, 6, 1, 7, 0)
 PLANE = 16
-LAG = 5
-LEAD = 4
 
 PAIRS = [(i, j) for i in range(3) for j in range(i, 3)]
 AT_AN, AT_AM, AT_NN, AT_NM, AT_B = 6, 15, 18, 24, 32
@@ -72,7 +70,7 @@
     dest_hbm, scan_hbm, src_hbm, mat_hbm, tp_hbm, tn_hbm, out_ref,
     dest_v, scan_s, src_v, mat_v, tp_v, tn_v, inv_v, inv_s, table, rhs, held,
     send, relay, recv, ucat, sums, ret_send, ret_recv, total, total_far,
-    in_sem, inv_sem, send_sem, relay_sem, onward_sem, recv_sem,
+    ready_sem, in_sem, inv_sem, send_sem, relay_sem, onward_sem, recv_sem,
     ret_ssem, ret_rsem, far_ssem, far_rsem,
 ):
     me_grp, me = lax.axis_index("grp"), lax.axis_index("tile")
@@ -81,11 +79,20 @@
     spot = me % PLANE
 
     def in_plane(group, sign):
-        dx, dy = turn(group % 4), turn(group // 4)
+        half = group // 8
+        dx = turn((1 - half) * (group // 2) + half * (group % 4))
+        dy = (1 - half) * (2 + group % 2) + half * (3 - group // 4)
         return level + ((y + 4 + sign * dy) % 4) * 4 + (x + 4 + sign * dx) % 4
 
     def along_z(dz):
         return ((z + dz) % 8) * PLANE + spot
+
+    x_peers = [level + y * 4 + (x + at) % 4 for at in (2, 1, 3)]
+    y_peers = [level + ((y + at) % 4) * 4 + x for at in (2, 1, 3)]
+    barrier = pltpu.get_barrier_semaphore()
+    for peer in [along_z(dz) for dz in DZ_ORDER[:-1]] + y_peers + x_peers:
+        pl.semaphore_signal(barrier, 1, device_id={"tile": peer})
+    pl.semaphore_signal(barrier, 1, device_id={"grp": 1 - me_grp})
 
     copies = [
         pltpu.make_async_copy(s, d, in_sem.at[i])
@@ -95,17 +102,6 @@
     ]
     for copy in copies:
         copy.start()
-
-    barrier = pltpu.get_barrier_semaphore()
-    for dz in DZ_ORDER[:-1]:
-        pl.semaphore_signal(barrier, 1, device_id={"tile": along_z(dz)})
-
-    def announce(group, carry):
-        pl.semaphore_signal(barrier, 1, device_id={"tile": in_plane(group, 1)})
-        return carry
-
-    lax.fori_loop(0, 15, announce, 0, unroll=5)
-    pl.semaphore_signal(barrier, 1, device_id={"grp": 1 - me_grp})
 
     copies[0].wait()
     blocks = jnp.broadcast_to(dest_v[...], (LANES, LANES)).T
@@ -138,8 +134,10 @@
                 slots[r * 8 + 6 : r * 8 + 8, :] = (mat_v[block] * scale + base).astype(F32)
         return carry
 
-    lax.fori_loop(0, LEAD, pack, 0, unroll=2)
-    pl.semaphore_wait(barrier, 7 + 15 + 1)
+    lax.fori_loop(0, 8, pack, 0, unroll=2)
+    pl.semaphore_wait(barrier, 7 + 3 + 3 + 1)
+    for peer in x_peers:
+        pl.semaphore_signal(ready_sem, 1, device_id={"tile": peer})
 
     def rows_of(group, j=0, count=8):
         return pl.ds(pl.multiple_of(group * LANES, LANES) + j * 16, count * 16)
@@ -176,10 +174,10 @@
         plane_copy(send, relay, group, send_sem, relay_sem).start()
         return carry
 
-    lax.fori_loop(0, LEAD, issue, 0)
+    lax.fori_loop(0, 8, issue, 0)
     lax.fori_loop(8, 16, pack, 0, unroll=2)
+    pl.semaphore_wait(ready_sem, 3)
     lax.fori_loop(8, 15, issue_plane, 0)
-    lax.fori_loop(LEAD, 8, pack, 0, unroll=2)
 
     copies[4].wait()
     copies[5].wait()
@@ -284,43 +282,28 @@
             z_copy(relay, recv, group, j, onward_sem, recv_sem).start()
         recv[rows_of(group, 7, 1), :] = relay[rows_of(group, 7, 1), :]
 
-    def work(pair):
-        landed(recv, pair, recv_sem).wait()
-        landed(recv, pair + 8, recv_sem, 7).wait()
-        settle([pair, pair + 8])
-        give_back(pair)
-        give_back(pair + 8)
-
     def early(step, carry):
         onward(step)
         onward_z(step + 8)
-
-        @pl.when(step + LEAD < 8)
-        def _():
-            issue(step + LEAD, 0)
-
-        return carry
-
-    def early_and_work(step, carry):
-        early(step, carry)
-        work(step - LAG)
-        return carry
-
-    def late(pair, carry):
-        work(pair)
-        return carry
-
-    lax.fori_loop(0, LAG, early, 0)
-    lax.fori_loop(LAG, 7, early_and_work, 0)
+        return carry
+
+    def late(step, carry):
+        landed(recv, step + 1, recv_sem).wait()
+        landed(recv, step + 8, recv_sem, 7).wait()
+        settle([step + 1, step + 8])
+        give_back(step + 1)
+        give_back(step + 8)
+        return carry
+
+    lax.fori_loop(0, 7, early, 0)
     onward(7)
     for j in range(7):
         z_copy(send, recv, 15, j, send_sem, recv_sem).start()
     recv[rows_of(15, 7, 1), :] = send[rows_of(15, 7, 1), :]
-    lax.fori_loop(7 - LAG, 6, late, 0)
-    landed(recv, 7, recv_sem).wait()
-    settle([7])
-    give_back(7)
-    lax.fori_loop(6, 7, late, 0)
+    landed(recv, 0, recv_sem).wait()
+    settle([0])
+    give_back(0)
+    lax.fori_loop(0, 7, late, 0)
     landed(recv, 15, recv_sem, 7).wait()
     settle([15])
     give_back(15, 7)
@@ -394,6 +377,7 @@
             vmem((TILES, 1, LANES), F32),
             vmem((32, LANES), F32),
             vmem((32, LANES), F32),
+            pltpu.SemaphoreType.REGULAR,
             dma((6,)),
             dma,
             dma,

time: 47.3 us -> 44.7 us (0.945)
  Pallas kernels: 45.9 us -> 43.3 us
    pallas_call x1, Pallas kernels: 45.9 us -> 43.3 us  [body(): pl.pallas_call(kernel, name='icp_step', out_shape=jax.ShapeDtypeStruct((8...]
where the time goes in v3:
time: 44.7 us; the launch traced here: 44.6 us
  Pallas kernels  43.3 us (97%)
  local copies, waits for them, and re-layouts  1.28 us (3%)
    pallas_call x1, Pallas kernels, body(): pl.pallas_call(kernel, name='icp_step', out_shape=jax.ShapeDtypeStruct((8...  43.3 us
    unnamed x1, local copies, waits for them, and re-layouts  1.28 us

profile of v3, /device:TPU:1, one launch (start us, length us, event | category | flops | bytes accessed | tf_op | source)
XLA Modules:
  0.0 44.6 jit_solution(12817979109673627940)
XLA Ops:
  0.0 43.3 %icp_step.1 = f32[8,128]{1,0:T(8,128)} custom-call(s32[1,128]{1,0:T(1,128)} %bitcast.7, s32[1,128]{1,0:T(1,128)} %scan_hbm.1, f32[384,2,128]{2,1,0:T(2,128)} %bitcast.4, s32[128,2,128]{2,1,0:T(2,128)} %bitcast.5, f32[3,32768]{1,0:T(4,128)} %tp_hbm.1, f32[3,32768]{1,0:T(4,128)} %tn_hbm.1), custom_call_target="tpu_custom_call" | custom-call | tf_op jit(solution)/shard_map/icp_step/pallas_call | solution.py:353
  43.3 1.3 %copy.8 = f32[6,64]{1,0:T(8,128)} copy(f32[6,64]{1,0:T(8,128)} %bitcast.6) | data formatting | bytes 3072

commit v4 on v3

--- a/solution.py
+++ b/solution.py
@@ -134,7 +134,7 @@
                 slots[r * 8 + 6 : r * 8 + 8, :] = (mat_v[block] * scale + base).astype(F32)
         return carry
 
-    lax.fori_loop(0, 8, pack, 0, unroll=2)
+    lax.fori_loop(0, 2, pack, 0, unroll=2)
     pl.semaphore_wait(barrier, 7 + 3 + 3 + 1)
     for peer in x_peers:
         pl.semaphore_signal(ready_sem, 1, device_id={"tile": peer})
@@ -174,7 +174,12 @@
         plane_copy(send, relay, group, send_sem, relay_sem).start()
         return carry
 
-    lax.fori_loop(0, 8, issue, 0)
+    def pack_and_issue(group, carry):
+        pack(group, carry)
+        return issue(group, carry)
+
+    lax.fori_loop(0, 2, issue, 0)
+    lax.fori_loop(2, 8, pack_and_issue, 0)
     lax.fori_loop(8, 16, pack, 0, unroll=2)
     pl.semaphore_wait(ready_sem, 3)
     lax.fori_loop(8, 15, issue_plane, 0)
@@ -389,7 +394,7 @@
             dma,
             dma,
         ],
-        compiler_params=pltpu.CompilerParams(collective_id=0, has_side_effects=True),
+        compiler_params=pltpu.CompilerParams(collective_id=0, has_side_effects=True, vmem_limit_bytes=56480000),
     )(
         intersection.reshape(1, TILES),
         target_scan,

time: 44.7 us -> 44.1 us (0.987)
  Pallas kernels: 43.3 us -> 42.7 us
    pallas_call x1, Pallas kernels: 43.3 us -> 42.7 us  [body(): pl.pallas_call(kernel, name='icp_step', out_shape=jax.ShapeDtypeStruct((8...]
    unnamed x1 -> x5, local copies, waits for them, and re-layouts: 1.28 us -> 1.26 us
where the time goes in v4:
time: 44.1 us; the launch traced here: 44 us
  Pallas kernels  42.7 us (97%)
  local copies, waits for them, and re-layouts  1.26 us (3%)
    pallas_call x1, Pallas kernels, body(): pl.pallas_call(kernel, name='icp_step', out_shape=jax.ShapeDtypeStruct((8...  42.7 us
    unnamed x5, local copies, waits for them, and re-layouts  1.26 us

profile of v4, /device:TPU:1, one launch (start us, length us, event | category | flops | bytes accessed | tf_op | source)
XLA Modules:
  0.0 44.0 jit_solution(12909008233044762808)
XLA Ops:
  0.0 0.0 copy-start
  0.0 0.0 copy-start.1
  0.0 0.7 %copy-done = s32[1,128,1]{1,2,0:T(1,128)S(1)} copy-done((s32[1,128,1]{1,2,0:T(1,128)S(1)}, s32[1,128,1]{1,2,0:T(1,128)}, u32[]{:S(2)}) %copy-start) | copy-done | bytes 536
  0.7 0.0 copy-done.1
  0.7 42.7 %icp_step.1 = f32[8,128]{1,0:T(8,128)S(1)} custom-call(s32[1,128]{1,0:T(1,128)S(1)} %bitcast.5, s32[1,128]{1,0:T(1,128)S(1)} %copy-done.1, f32[384,2,128]{2,1,0:T(2,128)} %bitcast.6, s32[128,2,128]{2,1,0:T(2,128)} %bitcast.7, f32[3,32768]{1,0:T(4,128)} %tp_hbm.1, f32[3,32768]{1,0:T(4,128)} %tn_hbm.1), custom_call_target="tpu_custom_call" | custom-call | tf_op jit(solution)/shard_map/icp_step/pallas_call | solution.py:358
  43.4 0.6 %copy.8 = f32[6,64]{1,0:T(8,128)} copy(f32[6,64]{1,0:T(8,128)S(1)} %bitcast.4) | data formatting | bytes 3072
Async XLA Ops:
  0.0 0.7 %copy-start = (s32[1,128,1]{1,2,0:T(1,128)S(1)}, s32[1,128,1]{1,2,0:T(1,128)}, u32[]{:S(2)}) copy-start(s32[1,128,1]{1,2,0:T(1,128)} %param.7) | copy-start | bytes 1540
  0.0 0.7 %copy-start.1 = (s32[1,128]{1,0:T(1,128)S(1)}, s32[1,128]{1,0:T(1,128)}, u32[]{:S(2)}) copy-start(s32[1,128]{1,0:T(1,128)} %scan_hbm.1) | copy-start | bytes 1540

commit v5 on v4

--- a/solution.py
+++ b/solution.py
@@ -87,13 +87,6 @@
     def along_z(dz):
         return ((z + dz) % 8) * PLANE + spot
 
-    x_peers = [level + y * 4 + (x + at) % 4 for at in (2, 1, 3)]
-    y_peers = [level + ((y + at) % 4) * 4 + x for at in (2, 1, 3)]
-    barrier = pltpu.get_barrier_semaphore()
-    for peer in [along_z(dz) for dz in DZ_ORDER[:-1]] + y_peers + x_peers:
-        pl.semaphore_signal(barrier, 1, device_id={"tile": peer})
-    pl.semaphore_signal(barrier, 1, device_id={"grp": 1 - me_grp})
-
     copies = [
         pltpu.make_async_copy(s, d, in_sem.at[i])
         for i, (s, d) in enumerate(
@@ -102,6 +95,13 @@
     ]
     for copy in copies:
         copy.start()
+
+    x_peers = [level + y * 4 + (x + at) % 4 for at in (2, 1, 3)]
+    y_peers = [level + ((y + at) % 4) * 4 + x for at in (2, 1, 3)]
+    barrier = pltpu.get_barrier_semaphore()
+    for peer in [along_z(dz) for dz in DZ_ORDER[:-1]] + y_peers + x_peers:
+        pl.semaphore_signal(barrier, 1, device_id={"tile": peer})
+    pl.semaphore_signal(barrier, 1, device_id={"grp": 1 - me_grp})
 
     copies[0].wait()
     blocks = jnp.broadcast_to(dest_v[...], (LANES, LANES)).T

time: 44.1 us -> 44.1 us (level)
  no operation moved by 1% of the time
where the time goes in v5:
time: 44.1 us; the launch traced here: 44 us
  Pallas kernels  42.8 us (97%)
  local copies, waits for them, and re-layouts  1.26 us (3%)
    pallas_call x1, Pallas kernels, body(): pl.pallas_call(kernel, name='icp_step', out_shape=jax.ShapeDtypeStruct((8...  42.8 us
    unnamed x5, local copies, waits for them, and re-layouts  1.26 us

profile of v5, /device:TPU:1, one launch (start us, length us, event | category | flops | bytes accessed | tf_op | source)
XLA Modules:
  0.0 44.0 jit_solution(15671320403525355130)
XLA Ops:
  0.0 0.0 copy-start
  0.0 0.0 copy-start.1
  0.0 0.7 %copy-done = s32[1,128,1]{1,2,0:T(1,128)S(1)} copy-done((s32[1,128,1]{1,2,0:T(1,128)S(1)}, s32[1,128,1]{1,2,0:T(1,128)}, u32[]{:S(2)}) %copy-start) | copy-done | bytes 536
  0.7 0.0 copy-done.1
  0.7 42.8 %icp_step.1 = f32[8,128]{1,0:T(8,128)S(1)} custom-call(s32[1,128]{1,0:T(1,128)S(1)} %bitcast.5, s32[1,128]{1,0:T(1,128)S(1)} %copy-done.1, f32[384,2,128]{2,1,0:T(2,128)} %bitcast.6, s32[128,2,128]{2,1,0:T(2,128)} %bitcast.7, f32[3,32768]{1,0:T(4,128)} %tp_hbm.1, f32[3,32768]{1,0:T(4,128)} %tn_hbm.1), custom_call_target="tpu_custom_call" | custom-call | tf_op jit(solution)/shard_map/icp_step/pallas_call | solution.py:358
  43.4 0.6 %copy.8 = f32[6,64]{1,0:T(8,128)} copy(f32[6,64]{1,0:T(8,128)S(1)} %bitcast.4) | data formatting | bytes 3072
Async XLA Ops:
  0.0 0.7 %copy-start = (s32[1,128,1]{1,2,0:T(1,128)S(1)}, s32[1,128,1]{1,2,0:T(1,128)}, u32[]{:S(2)}) copy-start(s32[1,128,1]{1,2,0:T(1,128)} %param.7) | copy-start | bytes 1540
  0.0 0.7 %copy-start.1 = (s32[1,128]{1,0:T(1,128)S(1)}, s32[1,128]{1,0:T(1,128)}, u32[]{:S(2)}) copy-start(s32[1,128]{1,0:T(1,128)} %scan_hbm.1) | copy-start | bytes 1540
